TPU v7x, 32 devices: a whole 2x2x4 slice. The times are simulated.
32 devices in a mesh: grp: 4 (over y, x), col: 8 (over z, core).
Axes of the slice: x: 2, y: 2, z: 4, core: 2. Of those that a mesh axis runs over, the one named last changes fastest.
Arguments:
- panels: bfloat16 [32, 4, 512, 512], P('col', None, 'grp'), may hold values from -1.296875 to 1.296875
- parent: float32 [32, 512, 512], P('col', 'grp'), may hold values from -6 to 6
- src_block: int32 [8, 40], P('col'), may hold values from 0 to 39, each once within a row
- dest_owner: int32 [320, 1], P('col'), may hold values from 0 to 7; in each aligned block of 40 rows (0 to 39, 40 to 79, ...) at most 7 rows name the same one
- target: int32 [320], P('col'), may hold values from 0 to 3
- counts: int32 [8], P('col'), may hold values from 20 to 40, as said below
Outputs:
- assembled: float32 [32, 512, 512], P('col', 'grp')
Inputs may be any that keep to these rules, and one draw needn't show every extreme that they name: `src_block`: each row of a column rank is a permutation of the 40 block pairs. `dest_owner`: among the 40 slots of one column rank at most 7 name the same owner. The live slots of a rank are its first counts[c]; some rank has all 40 live.
All inputs are finite; a program needn't handle non-finite values.
Results may differ from a plain program's by a relative error of at most 0.0026.
Values may be sent and summed in bfloat16 or wider, within the bound.
A program may use at most 128 MiB of HBM per device.

v0:
```python
import jax
import jax.numpy as jnp
import numpy as np
from jax import lax
from jax.sharding import PartitionSpec as P


def place_slots(src_block, dest_owner, target, counts, peer_count, capacity):
    slot_count = src_block.shape[1]
    slot_index = jnp.arange(slot_count, dtype=jnp.int32)
    owner_rank = dest_owner[:, 0]
    matches = (owner_rank[:, None] == jnp.arange(peer_count, dtype=jnp.int32)[None, :]).astype(
        jnp.int32
    )
    earlier = jnp.cumsum(matches, axis=0) - matches
    rank_in = jnp.sum(earlier * matches, axis=1)
    position = owner_rank * capacity + rank_in
    is_live = slot_index < counts[0]
    routed = jnp.zeros((peer_count * capacity,), jnp.int32).at[position].set(target)
    return (src_block[0], position, is_live, routed.reshape(peer_count, capacity))


def pack_updates(flat_updates, chosen, position, is_live, peer_count, capacity):
    picked = flat_updates[chosen]
    picked = jnp.where(is_live[:, None, None], picked, jnp.zeros_like(picked))
    buffer = (
        jnp.zeros((peer_count * capacity,) + picked.shape[1:], picked.dtype)
        .at[position]
        .set(picked)
    )
    return buffer.reshape((peer_count, capacity) + picked.shape[1:])


def assemble(received, labels, targets):
    arrived = received.reshape((-1,) + received.shape[2:])
    flat_labels = labels.reshape(-1)
    select = (flat_labels[None, :] == jnp.arange(targets, dtype=jnp.int32)[:, None]).astype(
        jnp.bfloat16
    )
    return jnp.einsum("tn,nrc->trc", select, arrived, preferred_element_type=jnp.float32)


def pair_products(own_rows, piece_rows):
    blocks = own_rows.shape[1]
    upper_table = np.array([a for a in range(blocks) for b in range(a + 1)], np.int32)
    lower_table = np.array([b for a in range(blocks) for b in range(a + 1)], np.int32)
    left_rows = own_rows[:, upper_table]
    right_rows = piece_rows[:, lower_table]
    return jnp.einsum(
        "fprw,fpcw->fprc", left_rows, right_rows, preferred_element_type=jnp.float32
    ).astype(jnp.bfloat16)


def per_device(panels, parent, src_block, dest_owner, target, counts):
    fronts, blocks, quarter, _ = panels.shape
    pair_count = blocks * (blocks + 1) // 2
    peer_count = lax.axis_size("col")
    slot_count = src_block.shape[1]
    capacity = (slot_count + peer_count - 1) // peer_count + slot_count // (2 * peer_count)
    targets = parent.shape[0]
    chosen, position, is_live, routed = place_slots(
        src_block, dest_owner, target, counts, peer_count, capacity
    )
    products = pair_products(panels, lax.all_gather(panels, "grp", axis=2, tiled=True))
    flat_updates = products.reshape(fronts * pair_count, quarter, products.shape[3])
    buffer = pack_updates(flat_updates, chosen, position, is_live, peer_count, capacity)
    received, labels = (
        lax.all_to_all(buffer, "col", split_axis=0, concat_axis=0, tiled=True),
        lax.all_to_all(routed, "col", split_axis=0, concat_axis=0, tiled=True),
    )
    return parent - assemble(received, labels, targets)


def solution(mesh):
    placed = (
        P("col", None, "grp", None),
        P("col", "grp", None),
        P("col", None),
        P("col", None),
        P("col"),
        P("col"),
    )
    return jax.shard_map(
        per_device, mesh=mesh, in_specs=placed, out_specs=P("col", "grp", None), check_vma=False
    )
```

profile of v0, /device:TPU:0, one launch (start us, length us, event | category | flops | bytes accessed | tf_op | source)
XLA Modules:
  0.0 359.7 jit_solution(15469304711273730429)
XLA Ops:
  6.5 0.0 all-gather.2.cloned.1.call-start
  6.5 0.7 all-gather.2.cloned.1.call-update
  7.3 0.7 fusion.12
  8.0 0.1 reduce_window_sum.11
  8.1 0.8 select_reduce_fusion
  8.9 0.7 fusion.16
  9.6 0.8 scatter_custom_fusion
  10.4 0.7 all_to_all.9
  11.1 6.4 %all-to-all-start = ((s32[8,1,7]{2,1,0:T(1,128)}), s32[8,1,7]{2,1,0:T(1,128)S(1)}, u32[]{:S(2)}, u32[]{:S(2)}) async-start(s32[8,1,7]{2,1,0:T(1,128)} %bitcast.3), calls=%async_computation | async-start | bytes 8192 | tf_op jit(solution)/shard_map/all_to_all | solution.py:69
  17.4 0.7 pad_clamp_fusion.2
  18.1 5.8 %gather_fusion = bf16[10,4,128,512]{3,2,1,0:T(8,128)(2,1)} fusion(bf16[4,4,128,512]{3,2,1,0:T(8,128)(2,1)} %param.10, s32[1024]{0:T(1024)S(1)} %pad_clamp_fusion.2), kind=kCustom, calls=%fused_computation | custom fusion | bytes 10485800 | tf_op jit(solution)/shard_map/gather | solution.py:47
  24.6 0.0 copy-done.1
  24.6 0.0 copy-done.2
  24.6 74.8 %all-gather.2.cloned.1.call-done = bf16[4,4,512,512]{3,2,1,0:T(8,128)(2,1)} async-done(((bf16[4,4,128,512]{3,2,1,0:T(8,128)(2,1)}), bf16[4,4,512,512]{3,2,1,0:T(8,128)(2,1)}) %all-gather.2.cloned.1.call-update) | async-done | bytes 8388624 | tf_op jit(solution)/shard_map/all_gather | solution.py:64
  99.4 6.0 %fusion.21 = (bf16[4,4,256,512]{3,2,1,0:T(8,128)(2,1)}, bf16[4,4,256,512]{3,2,1,0:T(8,128)(2,1)}) fusion(bf16[4,4,512,512]{3,2,1,0:T(8,128)(2,1)} %all-gather.2.cloned.1.call-done), kind=kLoop, calls=%fused_computation.36 | loop fusion | bytes 16777216 | tf_op jit(solution)/shard_map/gather | solution.py:48
  105.4 7.6 %gather_fusion.2 = bf16[10,4,256,512]{3,2,1,0:T(8,128)(2,1)} fusion(bf16[4,4,256,512]{3,2,1,0:T(8,128)(2,1)} %get-tuple-element.5, s32[1024]{0:T(1024)S(1)} %pad_clamp_fusion.1), kind=kCustom, calls=%fused_computation.2 | custom fusion | bytes 20971560 | tf_op jit(solution)/shard_map/gather | solution.py:48
  113.0 7.7 %gather_fusion.3 = bf16[10,4,256,512]{3,2,1,0:T(8,128)(2,1)} fusion(bf16[4,4,256,512]{3,2,1,0:T(8,128)(2,1)} %get-tuple-element.6, s32[1024]{0:T(1024)S(1)} %pad_clamp_fusion.1), kind=kCustom, calls=%fused_computation.3 | custom fusion | bytes 20971560 | tf_op jit(solution)/shard_map/gather | solution.py:48
  120.7 12.3 %copy_bitcast_fusion = (bf16[4,10,256,512]{3,2,1,0:T(8,128)(2,1)S(1)}, bf16[4,10,256,512]{3,2,1,0:T(8,128)(2,1)}) fusion(bf16[10,4,256,512]{3,2,1,0:T(8,128)(2,1)} %gather_fusion.3, bf16[10,4,256,512]{3,2,1,0:T(8,128)(2,1)} %gather_fusion.2), kind=kLoop, calls=%fused_computation.10 | loop fusion | bytes 41943040 | tf_op jit(solution)/shard_map/gather | solution.py:48
  133.1 10.5 %fusion.7 = bf16[4,10,128,512]{3,2,1,0:T(8,128)(2,1)} fusion(bf16[4,10,256,512]{3,2,1,0:T(8,128)(2,1)S(1)} %get-tuple-element.7, bf16[4,10,256,512]{3,2,1,0:T(8,128)(2,1)} %get-tuple-element.8, bf16[10,4,128,512]{3,2,1,0:T(8,128)(2,1)S(1)} %bitcast.30), kind=kOutput, calls=%fused_computation.16 | convolution fusion | flops 2728919040 | bytes 31457280 | tf_op jit(solution)/shard_map/fprw,fpcw->fprc/dot_general | solution.py:49
  143.6 7.1 %gather_fusion.1 = bf16[40,128,512]{2,1,0:T(8,128)(2,1)} fusion(bf16[40,128,512]{2,1,0:T(8,128)(2,1)} %bitcast.31, s32[1024]{0:T(1024)S(1)} %pad_clamp_fusion), kind=kCustom, calls=%fused_computation.1 | custom fusion | bytes 10485920 | tf_op jit(solution)/shard_map/gather | solution.py:24
  150.7 5.2 %broadcast_select_fusion = bf16[40,128,512]{2,1,0:T(8,128)(2,1)} fusion(bf16[40,128,512]{2,1,0:T(8,128)(2,1)} %gather_fusion.1, pred[40]{0:T(512)(128)(4,1)S(1)} %iota_compare_fusion.2), kind=kLoop, calls=%fused_computation.15 | loop fusion | flops 2621440 | bytes 10485800 | tf_op jit(solution)/shard_map/jit(_where)/select_n | solution.py:25
  155.8 3.8 %broadcast_in_dim.30 = bf16[56,128,512]{2,1,0:T(8,128)(2,1)} broadcast(bf16[]{:T(256)} %constant.12.clone.1), dimensions={} | broadcast | bytes 7340034 | tf_op jit(solution)/shard_map/broadcast_in_dim | solution.py:27
  159.7 14.1 %scatter_fusion = bf16[56,128,512]{2,1,0:T(8,128)(2,1)} fusion(bf16[56,128,512]{2,1,0:T(8,128)(2,1)} %broadcast_in_dim.30, s32[40]{0:T(128)S(1)} %fusion.16, bf16[40,128,512]{2,1,0:T(8,128)(2,1)} %broadcast_select_fusion), kind=kCustom, calls=%fused_computation.5 | custom fusion | bytes 15728800 | tf_op jit(solution)/shard_map/scatter | solution.py:29
  173.8 0.0 all-to-all-done
  173.8 5.0 %all-to-all-start.1 = ((bf16[8,7,128,512]{3,2,1,0:T(8,128)(2,1)}), bf16[8,7,128,512]{3,2,1,0:T(8,128)(2,1)}, u32[]{:S(2)}, u32[]{:S(2)}) async-start(bf16[8,7,128,512]{3,2,1,0:T(8,128)(2,1)} %bitcast.28), calls=%async_computation.1 | async-start | bytes 14680064 | tf_op jit(solution)/shard_map/all_to_all | solution.py:68
  178.8 0.0 copy-start
  178.8 0.5 broadcast.60
  179.3 0.7 reduce.3
  180.0 0.1 eq.34
  180.1 159.9 %all-to-all-done.1 = bf16[8,7,128,512]{3,2,1,0:T(8,128)(2,1)} async-done(((bf16[8,7,128,512]{3,2,1,0:T(8,128)(2,1)}), bf16[8,7,128,512]{3,2,1,0:T(8,128)(2,1)}, u32[]{:S(2)}, u32[]{:S(2)}) %all-to-all-start.1) | async-done | bytes 7340064 | tf_op jit(solution)/shard_map/all_to_all | solution.py:68
  340.0 11.5 %fusion.4 = f32[4,128,512]{2,0,1:T(4,128)S(1)} fusion(bf16[56,128,512]{2,1,0:T(8,128)(2,1)} %bitcast.13, s32[56]{0:T(128)S(1)} %eq.34), kind=kOutput, calls=%fused_computation.12 | convolution fusion | flops 29360352 | bytes 8388832 | tf_op jit(solution)/shard_map/tn,nrc->trc/dot_general | solution.py:40
  351.5 1.3 copy_subtract_fusion
  (12 shorter events, 0.0 us)
Async XLA Ops:
  6.5 18.0 %copy-start.1 = (s32[10]{0:T(128)S(1)}, s32[10]{0:T(128)}, u32[]{:S(2)}) copy-start(s32[10]{0:T(128)} %constant.35) | copy-start | bytes 124
  6.5 18.0 %copy-start.2 = (s32[1,40]{1,0:T(1,128)S(1)}, s32[1,40]{1,0:T(1,128)}, u32[]{:S(2)}) copy-start(s32[1,40]{1,0:T(1,128)} %param.12) | copy-start | bytes 484
  6.5 92.9 %all-gather.2.cloned.1.call-start = ((), (), s32[]{:S(2)}) async-start(), calls=%async_computation.2 | async-start | bytes 10485760 | tf_op jit(solution)/shard_map/all_gather | solution.py:64
  11.1 162.7 %all-to-all-start = ((s32[8,1,7]{2,1,0:T(1,128)}), s32[8,1,7]{2,1,0:T(1,128)S(1)}, u32[]{:S(2)}, u32[]{:S(2)}) async-start(s32[8,1,7]{2,1,0:T(1,128)} %bitcast.3), calls=%async_computation | async-start | bytes 8192 | tf_op jit(solution)/shard_map/all_to_all | solution.py:69
  113.0 20.0 %slice-start = ((s8[5242880]{0:T(1024)(128)(4,1)}), s8[1048576]{0:T(1024)(128)(4,1)S(1)}, s32[]{:S(2)}) async-start(s8[5242880]{0:T(1024)(128)(4,1)} %bitcast.29), calls=%async_computation.3 | async-start | bytes 2097152
  120.7 12.4 %slice-start.1 = ((s8[5242880]{0:T(1024)(128)(4,1)}), s8[4194304]{0:T(1024)(128)(4,1)S(1)}, s32[]{:S(2)}) async-start(s8[5242880]{0:T(1024)(128)(4,1)} %bitcast.29), calls=%async_computation.4 | async-start | bytes 8388608
  173.8 166.2 %all-to-all-start.1 = ((bf16[8,7,128,512]{3,2,1,0:T(8,128)(2,1)}), bf16[8,7,128,512]{3,2,1,0:T(8,128)(2,1)}, u32[]{:S(2)}, u32[]{:S(2)}) async-start(bf16[8,7,128,512]{3,2,1,0:T(8,128)(2,1)} %bitcast.28), calls=%async_computation.1 | async-start | bytes 14680064 | tf_op jit(solution)/shard_map/all_to_all | solution.py:68
  178.8 172.7 %copy-start = (f32[4,128,512]{2,1,0:T(8,128)S(1)}, f32[4,128,512]{2,1,0:T(8,128)}, u32[]{:S(2)}) copy-start(f32[4,128,512]{2,1,0:T(8,128)} %param.11) | copy-start | bytes 3145732
Sparse Core Ops, SparseCore 0:
  9.2 90.1 all-gather.1
where the time goes:
time: 360 us
  waiting for transfers between devices  235 us (65%)
  local copies, waits for them, and re-layouts  66.5 us (18%)
  matrix products  22 us (6%)
  between operations  14.1 us (4%)
  starting transfers between devices  11.4 us (3%)
  other arithmetic  10.2 us (3%)
    all_to_all x1, waiting for transfers between devices, per_device(): lax.all_to_all(buffer, 'col', split_axis=0, concat_axis=0, tiled=True)  160 us
    all_gather x1, waiting for transfers between devices, per_device(): lax.all_gather(panels, 'grp', axis=2, tiled=True)  74.8 us
    gather x4, local copies, waits for them, and re-layouts, pair_products(): right_rows = piece_rows[:, lower_table]  33.6 us
    scatter x1, local copies, waits for them, and re-layouts, pack_updates(): buffer = jnp.zeros((peer_count * capacity,) + picked.shape[1:], picked.dt...  14.1 us
    dot_general x1, matrix products, assemble(): jnp.einsum('tn,nrc->trc', select, arrived, preferred_element_type=jnp.flo...  11.5 us
    dot_general x1, matrix products, pair_products(): jnp.einsum('fprw,fpcw->fprc', left_rows, right_rows, preferred_element_ty...  10.5 us
  transfers between devices with their start and end apart: 3, of which 2 were waited for; matrix products, arithmetic and copies ran while one was open for 24% of the time, Pallas kernels for 0%

commit v1 on v0

--- a/solution.py
+++ b/solution.py
@@ -1,8 +1,14 @@
+import functools
+
 import jax
 import jax.numpy as jnp
 import numpy as np
 from jax import lax
+from jax.experimental import pallas as pl
+from jax.experimental.pallas import tpu as pltpu
 from jax.sharding import PartitionSpec as P
+
+MESH = pl.DeviceIdType.MESH
 
 
 def place_slots(src_block, dest_owner, target, counts, peer_count, capacity):
@@ -51,6 +57,216 @@
     ).astype(jnp.bfloat16)
 
 
+def slot_table(src_block, dest_owner, target, counts, peer_count, capacity):
+    slot_count = src_block.shape[1]
+    slot_index = jnp.arange(slot_count, dtype=jnp.int32)
+    owner = dest_owner[:, 0]
+    earlier = (slot_index[None, :] < slot_index[:, None]) & (owner[None, :] == owner[:, None])
+    rank_in = jnp.sum(earlier.astype(jnp.int32), axis=1)
+    position = owner * capacity + rank_in
+    hit = jnp.arange(peer_count * capacity, dtype=jnp.int32)[:, None] == position[None, :]
+    label = jnp.where(slot_index < counts[0], target + 1, 0)
+    pair = jnp.stack([src_block[0], label])
+    return jnp.sum(jnp.where(hit[None], pair[:, None, :], 0), axis=2)
+
+
+def kernel(
+    chips, capacity, table, own, parent, out,
+    from_x, from_y, from_d, product, kept, to_pair, from_pair, to_chip, from_chip,
+    x_send, x_recv, y_send, y_recv, dx_send, dx_recv, dy_send, dy_recv,
+    p_send, p_recv, z_send, z_recv,
+):
+    fronts, blocks, quarter, _ = own.shape
+    targets = parent.shape[0]
+    pairs = blocks * (blocks + 1) // 2
+    g, c = lax.axis_index("grp"), lax.axis_index("col")
+    gy, gx = g // 2, g % 2
+    z, core = c // 2, c % 2
+    x_peer = gy * 2 + (1 - gx)
+    y_peer = (1 - gy) * 2 + gx
+    d_peer = 3 - g
+    to_x, to_y = {"grp": x_peer, "col": c}, {"grp": y_peer, "col": c}
+    to_core = {"grp": g, "col": z * 2 + 1 - core}
+    far = [lax.rem(z + hop, chips) for hop in range(1, chips)]
+    to_far = [{"grp": g, "col": chip * 2 + core} for chip in far]
+
+    barrier = pltpu.get_barrier_semaphore()
+    peers = [to_x, to_y, to_core] + to_far
+    for peer in peers:
+        pl.semaphore_signal(barrier, inc=1, device_id=peer, device_id_type=MESH)
+    pl.semaphore_wait(barrier, len(peers))
+
+    def remote(src, dst, send, recv, device):
+        return pltpu.make_async_remote_copy(
+            src_ref=src, dst_ref=dst, send_sem=send, recv_sem=recv,
+            device_id=device, device_id_type=MESH,
+        )
+
+    half = fronts // 2
+    first, second = list(range(half)), list(range(half, fronts))
+    x_copy = [
+        remote(own.at[f], from_x.at[f], x_send.at[f], x_recv.at[f], to_x) for f in range(fronts)
+    ]
+    y_copy = [
+        remote(own.at[f], from_y.at[f], y_send.at[f], y_recv.at[f], to_y) for f in range(fronts)
+    ]
+    for f, h in zip(first + second, second + first):
+        x_copy[f].start()
+        y_copy[h].start()
+    dy_copy = [
+        remote(from_x.at[f], from_d.at[f], dy_send.at[f], dy_recv.at[f], to_y) for f in first
+    ]
+    dx_copy = [
+        remote(from_y.at[f], from_d.at[f], dx_send.at[f - half], dx_recv.at[f - half], to_x)
+        for f in second
+    ]
+
+    def products(rows):
+        def front(f, carry):
+            for b in range(blocks):
+                left = own[f, b:].reshape((blocks - b) * quarter, own.shape[3])
+                made = lax.dot_general(
+                    left, rows[f, b], (((1,), (1,)), ((), ())),
+                    preferred_element_type=jnp.float32,
+                ).astype(jnp.bfloat16)
+                for a in range(b, blocks):
+                    at = f * pairs + a * (a + 1) // 2 + b
+                    product[at] = made[(a - b) * quarter:(a - b + 1) * quarter]
+            return carry
+
+        lax.fori_loop(0, fronts, front, 0)
+
+    tile = 32
+
+    def select(parity, store):
+        def chip(zz, carry):
+            base = (zz * 2 + parity) * capacity
+            chosen = [table[0, base + k] for k in range(capacity)]
+            label = [table[1, base + k] for k in range(capacity)]
+            weight = [
+                [jnp.where(label[k] == t + 1, 1.0, 0.0).astype(jnp.float32) for t in range(targets)]
+                for k in range(capacity)
+            ]
+
+            def rows(i, carry):
+                at = pl.ds(pl.multiple_of(i * tile, tile), tile)
+                taken = [product[chosen[k], at, :].astype(jnp.float32) for k in range(capacity)]
+                for t in range(targets):
+                    total = taken[0] * weight[0][t]
+                    for k in range(1, capacity):
+                        total = total + taken[k] * weight[k][t]
+                    store(zz, t, at, total)
+                return carry
+
+            return lax.fori_loop(0, quarter // tile, rows, carry)
+
+        lax.fori_loop(0, chips, chip, 0)
+
+    def columns(member):
+        return pl.ds(pl.multiple_of(member * quarter, quarter), quarter)
+
+    p_copy = [
+        remote(to_pair.at[n], from_pair.at[n], p_send.at[n], p_recv.at[n], to_core)
+        for n in range(4)
+    ]
+    z_copy = [
+        [
+            remote(to_chip.at[n, h], from_chip.at[n, h], z_send.at[n, h], z_recv.at[n, h], to_far[h])
+            for h in range(chips - 1)
+        ]
+        for n in range(4)
+    ]
+
+    def chunk(n, rows, member):
+        products(rows)
+
+        def store_pair(zz, t, at, total):
+            to_pair[n, zz, t, at, :] = total.astype(jnp.bfloat16)
+
+        def store_kept(zz, t, at, total):
+            kept[zz, t, at, :] = total
+
+        select(1 - core, store_pair)
+        p_copy[n].start()
+        select(core, store_kept)
+        p_copy[n].wait_recv()
+        for h in range(chips - 1):
+            to_chip[n, h] = (kept[far[h]] + from_pair[n, far[h]].astype(jnp.float32)).astype(
+                jnp.bfloat16
+            )
+            z_copy[n][h].start()
+        at = columns(member)
+        out[:, :, at] = parent[:, :, at] - (kept[z] + from_pair[n, z].astype(jnp.float32))
+
+    def finish(n, member):
+        at = columns(member)
+        total = out[:, :, at]
+        for h in range(chips - 1):
+            z_copy[n][h].wait_recv()
+        for h in range(chips - 1):
+            total = total - from_chip[n, h].astype(jnp.float32)
+        out[:, :, at] = total
+
+    chunk(0, own, g)
+    for i in range(half):
+        x_copy[first[i]].wait_recv()
+        dy_copy[i].start()
+        y_copy[second[i]].wait_recv()
+        dx_copy[i].start()
+    finish(0, g)
+    for f in second:
+        x_copy[f].wait_recv()
+    chunk(1, from_x, x_peer)
+    for f in first:
+        y_copy[f].wait_recv()
+    chunk(2, from_y, y_peer)
+    for copy in dy_copy + dx_copy:
+        copy.wait_recv()
+    chunk(3, from_d, d_peer)
+    finish(1, x_peer)
+    finish(2, y_peer)
+    finish(3, d_peer)
+    for copy in x_copy + y_copy + dy_copy + dx_copy + p_copy:
+        copy.wait_send()
+    for row in z_copy:
+        for copy in row:
+            copy.wait_send()
+
+
+def fused(panels, parent, table, chips, capacity):
+    fronts, blocks, quarter, width = panels.shape
+    targets = parent.shape[0]
+    pairs = blocks * (blocks + 1) // 2
+    half = fronts // 2
+    rows = pltpu.VMEM(panels.shape, panels.dtype)
+    dma = pltpu.SemaphoreType.DMA
+    return pl.pallas_call(
+        functools.partial(kernel, chips, capacity),
+        out_shape=jax.ShapeDtypeStruct(parent.shape, parent.dtype),
+        in_specs=[
+            pl.BlockSpec(memory_space=pltpu.SMEM),
+            pl.BlockSpec(memory_space=pltpu.VMEM),
+            pl.BlockSpec(memory_space=pltpu.VMEM),
+        ],
+        out_specs=pl.BlockSpec(memory_space=pltpu.VMEM),
+        scratch_shapes=[
+            rows, rows, rows,
+            pltpu.VMEM((fronts * pairs, quarter, quarter), jnp.bfloat16),
+            pltpu.VMEM((chips, targets, quarter, quarter), jnp.float32),
+            pltpu.VMEM((4, chips, targets, quarter, quarter), jnp.bfloat16),
+            pltpu.VMEM((4, chips, targets, quarter, quarter), jnp.bfloat16),
+            pltpu.VMEM((4, chips - 1, targets, quarter, quarter), jnp.bfloat16),
+            pltpu.VMEM((4, chips - 1, targets, quarter, quarter), jnp.bfloat16),
+            dma((fronts,)), dma((fronts,)), dma((fronts,)), dma((fronts,)),
+            dma((half,)), dma((half,)), dma((half,)), dma((half,)),
+            dma((4,)), dma((4,)), dma((4, chips - 1)), dma((4, chips - 1)),
+        ],
+        compiler_params=pltpu.CompilerParams(
+            collective_id=0, has_side_effects=True, vmem_limit_bytes=60 * 1024 * 1024
+        ),
+    )(table, panels, parent)
+
+
 def per_device(panels, parent, src_block, dest_owner, target, counts):
     fronts, blocks, quarter, _ = panels.shape
     pair_count = blocks * (blocks + 1) // 2
@@ -58,6 +274,9 @@
     slot_count = src_block.shape[1]
     capacity = (slot_count + peer_count - 1) // peer_count + slot_count // (2 * peer_count)
     targets = parent.shape[0]
+    if lax.axis_size("grp") == 4 and peer_count % 2 == 0 and targets < capacity:
+        table = slot_table(src_block, dest_owner, target, counts, peer_count, capacity)
+        return fused(panels, parent, table, peer_count // 2, capacity)
     chosen, position, is_live, routed = place_slots(
         src_block, dest_owner, target, counts, peer_count, capacity
     )

time: 360 us -> 101 us (0.28)
  waiting for transfers between devices: 235 us -> 0 us
  Pallas kernels: 0 us -> 93.3 us
  local copies, waits for them, and re-layouts: 66.5 us -> 2.26 us
  matrix products: 22 us -> 0 us
  between operations: 14.1 us -> 0.66 us
  starting transfers between devices: 11.4 us -> 0 us
  other arithmetic: 10.2 us -> 3.63 us
    all_to_all x2 -> x0, waiting for transfers between devices: 160 us -> none  [the longest x1 160 us: per_device(): lax.all_to_all(buffer, 'col', split_axis=0, concat_axis=0, tiled=True)]
    pallas_call x0 -> x1, Pallas kernels: none -> 93.3 us  [fused(): pl.pallas_call(functools.partial(kernel, chips, capacity), out_shape=jax....]
    all_gather x1 -> x0, waiting for transfers between devices: 74.8 us -> none  [per_device(): lax.all_gather(panels, 'grp', axis=2, tiled=True)]
    gather x6 -> x0, local copies, waits for them, and re-layouts: 46.5 us -> none  [the longest x4 33.6 us: pair_products(): right_rows = piece_rows[:, lower_table]]
    dot_general x2 -> x0, matrix products: 22 us -> none  [the longest x1 11.5 us: assemble(): jnp.einsum('tn,nrc->trc', select, arrived, preferred_element_type=jnp.flo...]
    scatter x2 -> x0, local copies, waits for them, and re-layouts: 14.9 us -> none  [the longest x1 14.1 us: pack_updates(): buffer = jnp.zeros((peer_count * capacity,) + picked.shape[1:], picked.dt...]
    all_to_all x2 -> x0, starting transfers between devices: 11.4 us -> none  [the longest x1 6.35 us: per_device(): lax.all_to_all(routed, 'col', split_axis=0, concat_axis=0, tiled=True)]
    select_n x3 -> x0, other arithmetic: 5.86 us -> none  [the longest x1 5.18 us: pack_updates(): picked = jnp.where(is_live[:, None, None], picked, jnp.zeros_like(picked))]
  transfers between devices with their start and end apart: 3 -> 0, of which waited for: 2 -> 0; matrix products, arithmetic and copies ran while one was open for 24% -> 0% of each run, Pallas kernels for 0% -> 0%
where the time goes in v1:
time: 101 us; the launch traced here: 99.8 us
  Pallas kernels  93.3 us (92%)
  other arithmetic  3.63 us (4%)
  local copies, waits for them, and re-layouts  2.26 us (2%)
    pallas_call x1, Pallas kernels, fused(): pl.pallas_call(functools.partial(kernel, chips, capacity), out_shape=jax....  93.3 us
    unnamed x1, local copies, waits for them, and re-layouts  2.26 us

profile of v1, /device:TPU:0, one launch (start us, length us, event | category | flops | bytes accessed | tf_op | source)
XLA Modules:
  0.0 99.8 jit_solution(10572785171418239490)
XLA Ops:
  0.7 0.7 fusion.1
  1.3 0.7 pad_add_fusion
  2.0 0.9 convert_reduce_fusion
  2.9 0.7 multiply_add_fusion
  3.6 0.1 iota_compare_fusion.1
  3.6 0.7 select_reduce_fusion.table
  4.3 93.3 %shard_map.64 = f32[4,128,512]{2,1,0:T(8,128)} custom-call(s32[2,56]{1,0:T(2,128)} %select_reduce_fusion.table, bf16[4,4,128,512]{3,2,1,0:T(8,128)(2,1)} %own.1, f32[4,128,512]{2,1,0:T(8,128)} %parent.1), custom_call_target="tpu_custom_call" | custom-call | tf_op jit(solution)/shard_map/pallas_call | solution.py:243
  97.6 2.3 %copy.9 = f32[4,128,512]{2,1,0:T(8,128)} copy(f32[4,128,512]{2,1,0:T(8,128)} %shard_map.64) | data formatting | bytes 2097152

commit v2 on v0

--- a/solution.py
+++ b/solution.py
@@ -1,8 +1,14 @@
+import functools
+
 import jax
 import jax.numpy as jnp
 import numpy as np
 from jax import lax
+from jax.experimental import pallas as pl
+from jax.experimental.pallas import tpu as pltpu
 from jax.sharding import PartitionSpec as P
+
+MESH = pl.DeviceIdType.MESH
 
 
 def place_slots(src_block, dest_owner, target, counts, peer_count, capacity):
@@ -51,6 +57,271 @@
     ).astype(jnp.bfloat16)
 
 
+def kernel(
+    chips, capacity, split, src_block, owner, target, counts, own, parent, out,
+    table, from_x, from_y, product, kept, summed, to_pair, from_pair, to_chip, from_chip,
+    to_back, from_back,
+    x_send, x_recv, y_send, y_recv, p_send, p_recv, z_send, z_recv, b_send, b_recv,
+):
+    fronts, blocks, quarter, width = own.shape
+    targets = parent.shape[0]
+    pairs = blocks * (blocks + 1) // 2
+    slots = src_block.shape[1]
+    g, c = lax.axis_index("grp"), lax.axis_index("col")
+    gy, gx = g // 2, g % 2
+    z, core = c // 2, c % 2
+    x_peer = gy * 2 + (1 - gx)
+    y_peer = (1 - gy) * 2 + gx
+    d_peer = 3 - g
+    to_x, to_y = {"grp": x_peer, "col": c}, {"grp": y_peer, "col": c}
+    to_core = {"grp": g, "col": z * 2 + 1 - core}
+    far = [lax.rem(z + hop, chips) for hop in range(1, chips)]
+    to_far = [{"grp": g, "col": chip * 2 + core} for chip in far]
+
+    barrier = pltpu.get_barrier_semaphore()
+    peers = [to_x, to_y, to_core] + to_far
+    for peer in peers:
+        pl.semaphore_signal(barrier, inc=1, device_id=peer, device_id_type=MESH)
+    pl.semaphore_wait(barrier, len(peers))
+
+    def remote(src, dst, send, recv, device):
+        return pltpu.make_async_remote_copy(
+            src_ref=src, dst_ref=dst, send_sem=send, recv_sem=recv,
+            device_id=device, device_id_type=MESH,
+        )
+
+    piece = quarter // split
+    x_copy, y_copy = [], []
+    for k in range(split):
+        at = pl.ds(k * piece, piece)
+        x_copy.append(
+            remote(own.at[:, :, at], from_x[k], x_send.at[k], x_recv.at[k], to_x)
+        )
+        y_copy.append(
+            remote(own.at[:, :, at], from_y[k], y_send.at[k], y_recv.at[k], to_y)
+        )
+        x_copy[k].start()
+        y_copy[k].start()
+
+    def list_owner(o, carry):
+        def look(s, state):
+            count, chosen, label = state
+            mine = owner[0, s] == o
+            named = jnp.where(s < counts[0], target[0, s] + 1, 0)
+            hits = [jnp.logical_and(mine, count == k) for k in range(capacity)]
+            return (
+                count + jnp.where(mine, 1, 0),
+                tuple(jnp.where(hits[k], src_block[0, s], chosen[k]) for k in range(capacity)),
+                tuple(jnp.where(hits[k], named, label[k]) for k in range(capacity)),
+            )
+
+        none = tuple(jnp.int32(0) for _ in range(capacity))
+        _, chosen, label = lax.fori_loop(0, slots, look, (jnp.int32(0), none, none))
+        for k in range(capacity):
+            table[0, o * capacity + k] = chosen[k]
+            table[1, o * capacity + k] = label[k]
+        return carry
+
+    lax.fori_loop(0, 2 * chips, list_owner, 0)
+
+    def place(n, source, against, pieces):
+        high = quarter // pieces
+        share = len(source) // pieces
+        return [
+            (source[i * share:(i + 1) * share], high, against, n * quarter + i * high)
+            for i in range(pieces)
+        ]
+
+    units = (
+        place(0, [own], [own], 1)
+        + place(1, from_x, [own], split)
+        + place(2, from_y, [own], split)
+        + place(3, from_y, from_x, 2)
+    )
+    u_own, u_x, u_y = 0, list(range(1, 1 + split)), list(range(1 + split, 1 + 2 * split))
+    u_d = [1 + 2 * split, 2 + 2 * split]
+    tile = 32
+
+    p_copy, z_copy = [], []
+    for u in range(len(units)):
+        p_copy.append(remote(to_pair[u], from_pair[u], p_send.at[u], p_recv.at[u], to_core))
+        z_copy.append([
+            remote(
+                to_chip[u].at[h], from_chip[u].at[h],
+                z_send.at[u, h], z_recv.at[u, h], to_far[h],
+            )
+            for h in range(chips - 1)
+        ])
+
+    def select(high, parity, store):
+        def chip(zz, carry):
+            base = (zz * 2 + parity) * capacity
+            chosen = [table[0, base + k] for k in range(capacity)]
+            label = [table[1, base + k] for k in range(capacity)]
+            weight = [
+                [jnp.where(label[k] == t + 1, 1.0, 0.0).astype(jnp.float32) for t in range(targets)]
+                for k in range(capacity)
+            ]
+
+            def rows(i, carry):
+                start = pl.multiple_of(i * tile, tile)
+                taken = [
+                    product[chosen[k], pl.ds(start, tile), :].astype(jnp.float32)
+                    for k in range(capacity)
+                ]
+                for t in range(targets):
+                    total = taken[0] * weight[0][t]
+                    for k in range(1, capacity):
+                        total = total + taken[k] * weight[k][t]
+                    store(zz, t, start, total)
+                return carry
+
+            return lax.fori_loop(0, high // tile, rows, carry)
+
+        lax.fori_loop(0, chips, chip, 0)
+
+    def make(u, slot):
+        source, high, against, _ = units[u]
+
+        def front(f, carry):
+            for b in range(blocks):
+                left = jnp.concatenate([ref[f, b] for ref in source], axis=0)
+                right = jnp.concatenate(
+                    [ref[f, a] for a in range(b, blocks) for ref in against], axis=0
+                )
+                made = lax.dot_general(
+                    left, right, (((1,), (1,)), ((), ())),
+                    preferred_element_type=jnp.float32,
+                ).astype(jnp.bfloat16)
+                for a in range(b, blocks):
+                    at = f * pairs + a * (a + 1) // 2 + b
+                    product[at, :high] = made[:, (a - b) * quarter:(a - b + 1) * quarter]
+            return carry
+
+        lax.fori_loop(0, fronts, front, 0)
+
+        def store_pair(zz, t, start, total):
+            to_pair[u][zz, t, pl.ds(start, tile), :] = total.astype(jnp.bfloat16)
+
+        def store_kept(zz, t, start, total):
+            kept[slot, zz, t, pl.ds(start, tile), :] = total
+
+        select(high, 1 - core, store_pair)
+        p_copy[u].start()
+        select(high, core, store_kept)
+
+    def pass_on(u, slot):
+        _, high, _, row = units[u]
+        at = slice(row, row + high)
+        p_copy[u].wait_recv()
+        for h in range(chips - 1):
+            to_chip[u][h] = (
+                kept[slot, far[h], :, :high] + from_pair[u][far[h]].astype(jnp.float32)
+            ).astype(jnp.bfloat16)
+            z_copy[u][h].start()
+        summed[:, at] = kept[slot, z, :, :high] + from_pair[u][z].astype(jnp.float32)
+
+    def finish(u):
+        _, high, _, row = units[u]
+        at = slice(row, row + high)
+        for h in range(chips - 1):
+            z_copy[u][h].wait_recv()
+        total = summed[:, at]
+        for h in range(chips - 1):
+            total = total + from_chip[u][h].astype(jnp.float32)
+        return total
+
+    def settle(u):
+        _, high, _, row = units[u]
+        summed[:, row:row + high] = finish(u)
+
+    def write(member, total_of):
+        at = pl.ds(pl.multiple_of(member * quarter, quarter), quarter)
+        for t in range(targets):
+            out[t, :, at] = parent[t, :, at] - total_of(t).T
+
+    make(u_own, 0)
+    pass_on(u_own, 0)
+    for k in range(split - 1):
+        x_copy[k].wait_recv()
+        make(u_x[k], 0)
+        y_copy[k].wait_recv()
+        make(u_y[k], 1)
+        pass_on(u_x[k], 0)
+        pass_on(u_y[k], 1)
+    settle(u_own)
+    write(g, lambda t: summed[t, :quarter])
+    x_copy[-1].wait_recv()
+    y_copy[-1].wait_recv()
+    make(u_d[0], 0)
+    make(u_d[1], 1)
+    pass_on(u_d[0], 0)
+    make(u_x[-1], 0)
+    pass_on(u_d[1], 1)
+    make(u_y[-1], 1)
+    pass_on(u_x[-1], 0)
+    pass_on(u_y[-1], 1)
+    for k in range(split - 1):
+        settle(u_x[k])
+        settle(u_y[k])
+    for u in u_d:
+        row, high = units[u][3], units[u][1]
+        to_back[:, row - 3 * quarter:row - 3 * quarter + high] = finish(u)
+    back = remote(to_back, from_back, b_send, b_recv, to_x)
+    back.start()
+    settle(u_x[-1])
+    write(x_peer, lambda t: summed[t, quarter:2 * quarter])
+    settle(u_y[-1])
+    write(y_peer, lambda t: summed[t, 2 * quarter:3 * quarter])
+    back.wait_recv()
+    write(d_peer, lambda t: from_back[t])
+    for copy in x_copy + y_copy + p_copy + [back]:
+        copy.wait_send()
+    for row in z_copy:
+        for copy in row:
+            copy.wait_send()
+
+
+def fused(panels, parent, src_block, dest_owner, target, counts, chips, capacity):
+    fronts, blocks, quarter, width = panels.shape
+    targets = parent.shape[0]
+    pairs = blocks * (blocks + 1) // 2
+    split = 4
+    units = 3 + 2 * split
+    piece = pltpu.VMEM((fronts, blocks, quarter // split, width), panels.dtype)
+    heights = [quarter] + [quarter // split] * (2 * split) + [quarter // 2] * 2
+
+    def buffers(count):
+        return [pltpu.VMEM((count, targets, high, quarter), jnp.bfloat16) for high in heights]
+
+    last = (targets, quarter, quarter)
+    dma = pltpu.SemaphoreType.DMA
+    scalars = pl.BlockSpec(memory_space=pltpu.SMEM)
+    arrays = pl.BlockSpec(memory_space=pltpu.VMEM)
+    return pl.pallas_call(
+        functools.partial(kernel, chips, capacity, split),
+        out_shape=jax.ShapeDtypeStruct(parent.shape, parent.dtype),
+        in_specs=[scalars] * 4 + [arrays] * 2,
+        out_specs=arrays,
+        scratch_shapes=[
+            pltpu.SMEM((2, 2 * chips * capacity), jnp.int32),
+            [piece] * split, [piece] * split,
+            pltpu.VMEM((fronts * pairs, quarter, quarter), jnp.bfloat16),
+            pltpu.VMEM((2, chips) + last, jnp.float32),
+            pltpu.VMEM((targets, 4 * quarter, quarter), jnp.float32),
+            buffers(chips), buffers(chips), buffers(chips - 1), buffers(chips - 1),
+            pltpu.VMEM(last, jnp.float32),
+            pltpu.VMEM(last, jnp.float32),
+            dma((split,)), dma((split,)), dma((split,)), dma((split,)),
+            dma((units,)), dma((units,)), dma((units, chips - 1)), dma((units, chips - 1)),
+            dma, dma,
+        ],
+        compiler_params=pltpu.CompilerParams(
+            collective_id=0, has_side_effects=True, vmem_limit_bytes=60 * 1024 * 1024
+        ),
+    )(src_block, dest_owner.reshape(1, -1), target.reshape(1, -1), counts, panels, parent)
+
+
 def per_device(panels, parent, src_block, dest_owner, target, counts):
     fronts, blocks, quarter, _ = panels.shape
     pair_count = blocks * (blocks + 1) // 2
@@ -58,6 +329,10 @@
     slot_count = src_block.shape[1]
     capacity = (slot_count + peer_count - 1) // peer_count + slot_count // (2 * peer_count)
     targets = parent.shape[0]
+    if lax.axis_size("grp") == 4 and peer_count % 2 == 0 and targets < capacity:
+        return fused(
+            panels, parent, src_block, dest_owner, target, counts, peer_count // 2, capacity
+        )
     chosen, position, is_live, routed = place_slots(
         src_block, dest_owner, target, counts, peer_count, capacity
     )

time: 360 us -> 85.5 us (0.24)
  waiting for transfers between devices: 235 us -> 0 us
  Pallas kernels: 0 us -> 82.4 us
  local copies, waits for them, and re-layouts: 66.5 us -> 2.26 us
  matrix products: 22 us -> 0 us
  between operations: 14.1 us -> 0.66 us
  starting transfers between devices: 11.4 us -> 0 us
  other arithmetic: 10.2 us -> 0 us
    all_to_all x2 -> x0, waiting for transfers between devices: 160 us -> none  [the longest x1 160 us: per_device(): lax.all_to_all(buffer, 'col', split_axis=0, concat_axis=0, tiled=True)]
    pallas_call x0 -> x1, Pallas kernels: none -> 82.4 us  [fused(): pl.pallas_call(functools.partial(kernel, chips, capacity, split), out_sha...]
    all_gather x1 -> x0, waiting for transfers between devices: 74.8 us -> none  [per_device(): lax.all_gather(panels, 'grp', axis=2, tiled=True)]
    gather x6 -> x0, local copies, waits for them, and re-layouts: 46.5 us -> none  [the longest x4 33.6 us: pair_products(): right_rows = piece_rows[:, lower_table]]
    dot_general x2 -> x0, matrix products: 22 us -> none  [the longest x1 11.5 us: assemble(): jnp.einsum('tn,nrc->trc', select, arrived, preferred_element_type=jnp.flo...]
    scatter x2 -> x0, local copies, waits for them, and re-layouts: 14.9 us -> none  [the longest x1 14.1 us: pack_updates(): buffer = jnp.zeros((peer_count * capacity,) + picked.shape[1:], picked.dt...]
    all_to_all x2 -> x0, starting transfers between devices: 11.4 us -> none  [the longest x1 6.35 us: per_device(): lax.all_to_all(routed, 'col', split_axis=0, concat_axis=0, tiled=True)]
    select_n x3 -> x0, other arithmetic: 5.86 us -> none  [the longest x1 5.18 us: pack_updates(): picked = jnp.where(is_live[:, None, None], picked, jnp.zeros_like(picked))]
  transfers between devices with their start and end apart: 3 -> 0, of which waited for: 2 -> 0; matrix products, arithmetic and copies ran while one was open for 24% -> 0% of each run, Pallas kernels for 0% -> 0%
where the time goes in v2:
time: 85.5 us; the launch traced here: 85.3 us
  Pallas kernels  82.4 us (96%)
  local copies, waits for them, and re-layouts  2.26 us (3%)
    pallas_call x1, Pallas kernels, fused(): pl.pallas_call(functools.partial(kernel, chips, capacity, split), out_sha...  82.4 us
    unnamed x1, local copies, waits for them, and re-layouts  2.26 us

profile of v2, /device:TPU:0, one launch (start us, length us, event | category | flops | bytes accessed | tf_op | source)
XLA Modules:
  0.0 85.3 jit_solution(13455190765026833071)
XLA Ops:
  0.7 82.4 %shard_map.64 = f32[4,128,512]{2,1,0:T(8,128)} custom-call(s32[1,40]{1,0:T(1,128)} %src_block.1, s32[1,40]{1,0:T(1,128)} %bitcast.2, s32[1,40]{1,0:T(1,128)} %bitcast.3, s32[1]{0:T(128)S(6)} %copy.8.counts, bf16[4,4,128,512]{3,2,1,0:T(8,128)(2,1)} %own.1, f32[4,128,512]{2,1,0:T(8,128)} %parent.1), custom_call_target="tpu_custom_call" | custom-call | tf_op jit(solution)/shard_map/pallas_call | solution.py:301
  83.1 2.3 %copy.9 = f32[4,128,512]{2,1,0:T(8,128)} copy(f32[4,128,512]{2,1,0:T(8,128)} %shard_map.64) | data formatting | bytes 2097152

commit v3 on v2

--- a/solution.py
+++ b/solution.py
@@ -134,12 +134,13 @@
 
     units = (
         place(0, [own], [own], 1)
-        + place(1, from_x, [own], split)
-        + place(2, from_y, [own], split)
+        + [
+            ([from_x[k], from_y[k]], 2 * piece, [own], quarter + k * 2 * piece)
+            for k in range(split)
+        ]
         + place(3, from_y, from_x, 2)
     )
-    u_own, u_x, u_y = 0, list(range(1, 1 + split)), list(range(1 + split, 1 + 2 * split))
-    u_d = [1 + 2 * split, 2 + 2 * split]
+    u_own, u_near, u_d = 0, list(range(1, 1 + split)), [1 + split, 2 + split]
     tile = 32
 
     p_copy, z_copy = [], []
@@ -180,7 +181,7 @@
 
         lax.fori_loop(0, chips, chip, 0)
 
-    def make(u, slot):
+    def make(u):
         source, high, against, _ = units[u]
 
         def front(f, carry):
@@ -204,22 +205,22 @@
             to_pair[u][zz, t, pl.ds(start, tile), :] = total.astype(jnp.bfloat16)
 
         def store_kept(zz, t, start, total):
-            kept[slot, zz, t, pl.ds(start, tile), :] = total
+            kept[zz, t, pl.ds(start, tile), :] = total
 
         select(high, 1 - core, store_pair)
         p_copy[u].start()
         select(high, core, store_kept)
 
-    def pass_on(u, slot):
+    def pass_on(u):
         _, high, _, row = units[u]
         at = slice(row, row + high)
         p_copy[u].wait_recv()
         for h in range(chips - 1):
             to_chip[u][h] = (
-                kept[slot, far[h], :, :high] + from_pair[u][far[h]].astype(jnp.float32)
+                kept[far[h], :, :high] + from_pair[u][far[h]].astype(jnp.float32)
             ).astype(jnp.bfloat16)
             z_copy[u][h].start()
-        summed[:, at] = kept[slot, z, :, :high] + from_pair[u][z].astype(jnp.float32)
+        summed[:, at] = kept[z, :, :high] + from_pair[u][z].astype(jnp.float32)
 
     def finish(u):
         _, high, _, row = units[u]
@@ -240,42 +241,38 @@
         for t in range(targets):
             out[t, :, at] = parent[t, :, at] - total_of(t).T
 
-    make(u_own, 0)
-    pass_on(u_own, 0)
+    def near(first):
+        parts = [slice(units[u][3] + first, units[u][3] + first + piece) for u in u_near]
+        return lambda t: jnp.concatenate([summed[t, part] for part in parts], axis=0)
+
+    make(u_own)
+    pass_on(u_own)
     for k in range(split - 1):
         x_copy[k].wait_recv()
-        make(u_x[k], 0)
         y_copy[k].wait_recv()
-        make(u_y[k], 1)
-        pass_on(u_x[k], 0)
-        pass_on(u_y[k], 1)
+        make(u_near[k])
+        pass_on(u_near[k])
     settle(u_own)
     write(g, lambda t: summed[t, :quarter])
     x_copy[-1].wait_recv()
     y_copy[-1].wait_recv()
-    make(u_d[0], 0)
-    make(u_d[1], 1)
-    pass_on(u_d[0], 0)
-    make(u_x[-1], 0)
-    pass_on(u_d[1], 1)
-    make(u_y[-1], 1)
-    pass_on(u_x[-1], 0)
-    pass_on(u_y[-1], 1)
+    for u in u_d + u_near[-1:]:
+        make(u)
+        pass_on(u)
     for k in range(split - 1):
-        settle(u_x[k])
-        settle(u_y[k])
-    for u in u_d:
-        row, high = units[u][3], units[u][1]
-        to_back[:, row - 3 * quarter:row - 3 * quarter + high] = finish(u)
-    back = remote(to_back, from_back, b_send, b_recv, to_x)
-    back.start()
-    settle(u_x[-1])
-    write(x_peer, lambda t: summed[t, quarter:2 * quarter])
-    settle(u_y[-1])
-    write(y_peer, lambda t: summed[t, 2 * quarter:3 * quarter])
-    back.wait_recv()
-    write(d_peer, lambda t: from_back[t])
-    for copy in x_copy + y_copy + p_copy + [back]:
+        settle(u_near[k])
+    back = []
+    for i, u in enumerate(u_d):
+        to_back[i][...] = finish(u)
+        back.append(remote(to_back[i], from_back[i], b_send.at[i], b_recv.at[i], to_x))
+        back[i].start()
+    settle(u_near[-1])
+    write(x_peer, near(0))
+    write(y_peer, near(piece))
+    for copy in back:
+        copy.wait_recv()
+    write(d_peer, lambda t: jnp.concatenate([ref[t] for ref in from_back], axis=0))
+    for copy in x_copy + y_copy + p_copy + back:
         copy.wait_send()
     for row in z_copy:
         for copy in row:
@@ -287,14 +284,15 @@
     targets = parent.shape[0]
     pairs = blocks * (blocks + 1) // 2
     split = 4
-    units = 3 + 2 * split
+    units = 3 + split
     piece = pltpu.VMEM((fronts, blocks, quarter // split, width), panels.dtype)
-    heights = [quarter] + [quarter // split] * (2 * split) + [quarter // 2] * 2
+    heights = [quarter] + [2 * quarter // split] * split + [quarter // 2] * 2
 
     def buffers(count):
         return [pltpu.VMEM((count, targets, high, quarter), jnp.bfloat16) for high in heights]
 
     last = (targets, quarter, quarter)
+    half = pltpu.VMEM((targets, quarter // 2, quarter), jnp.float32)
     dma = pltpu.SemaphoreType.DMA
     scalars = pl.BlockSpec(memory_space=pltpu.SMEM)
     arrays = pl.BlockSpec(memory_space=pltpu.VMEM)
@@ -307,14 +305,13 @@
             pltpu.SMEM((2, 2 * chips * capacity), jnp.int32),
             [piece] * split, [piece] * split,
             pltpu.VMEM((fronts * pairs, quarter, quarter), jnp.bfloat16),
-            pltpu.VMEM((2, chips) + last, jnp.float32),
+            pltpu.VMEM((chips,) + last, jnp.float32),
             pltpu.VMEM((targets, 4 * quarter, quarter), jnp.float32),
             buffers(chips), buffers(chips), buffers(chips - 1), buffers(chips - 1),
-            pltpu.VMEM(last, jnp.float32),
-            pltpu.VMEM(last, jnp.float32),
+            [half, half], [half, half],
             dma((split,)), dma((split,)), dma((split,)), dma((split,)),
             dma((units,)), dma((units,)), dma((units, chips - 1)), dma((units, chips - 1)),
-            dma, dma,
+            dma((2,)), dma((2,)),
         ],
         compiler_params=pltpu.CompilerParams(
             collective_id=0, has_side_effects=True, vmem_limit_bytes=60 * 1024 * 1024

time: 85.5 us -> 82.1 us (0.960)
  Pallas kernels: 82.4 us -> 79.1 us
    pallas_call x1, Pallas kernels: 82.4 us -> 79.1 us  [fused(): pl.pallas_call(functools.partial(kernel, chips, capacity, split), out_sha...]
where the time goes in v3:
time: 82.1 us; the launch traced here: 82 us
  Pallas kernels  79.1 us (96%)
  local copies, waits for them, and re-layouts  2.26 us (3%)
    pallas_call x1, Pallas kernels, fused(): pl.pallas_call(functools.partial(kernel, chips, capacity, split), out_sha...  79.1 us
    unnamed x1, local copies, waits for them, and re-layouts  2.26 us

profile of v3, /device:TPU:0, one launch (start us, length us, event | category | flops | bytes accessed | tf_op | source)
XLA Modules:
  0.0 82.0 jit_solution(17389685602503184483)
XLA Ops:
  0.7 79.1 %shard_map.64 = f32[4,128,512]{2,1,0:T(8,128)} custom-call(s32[1,40]{1,0:T(1,128)} %src_block.1, s32[1,40]{1,0:T(1,128)} %bitcast.2, s32[1,40]{1,0:T(1,128)} %bitcast.3, s32[1]{0:T(128)S(6)} %copy.8.counts, bf16[4,4,128,512]{3,2,1,0:T(8,128)(2,1)} %own.1, f32[4,128,512]{2,1,0:T(8,128)} %parent.1), custom_call_target="tpu_custom_call" | custom-call | tf_op jit(solution)/shard_map/pallas_call | solution.py:299
  79.7 2.3 %copy.9 = f32[4,128,512]{2,1,0:T(8,128)} copy(f32[4,128,512]{2,1,0:T(8,128)} %shard_map.64) | data formatting | bytes 2097152
